TPU v7x, 32 devices: a whole 2x2x4 slice. The times are simulated.
32 devices in a mesh: chan: 4 (over x, core), az: 8 (over z, y).
Axes of the slice: x: 2, y: 2, z: 4, core: 2. Of those that a mesh axis runs over, the one named last changes fastest.
Arguments:
- signal: bfloat16 [4, 2, 128, 8192], P('chan', None, 'az'), may hold values from -6 to 6
- tap_table: float32 [64, 16], replicated, may hold values from -1.5 to 1.5
- range_shift: int32 [1024], P('az'), may hold values from -8 to 8
- tap_index: int32 [1024], P('az'), may hold values from 0 to 63
- ref_channel: int32 [8], P('az'), may hold values from 0 to 3
Outputs:
- picture: float32 [4, 2, 128, 1024], P('chan', None, None, 'az')
All inputs are finite; a program needn't handle non-finite values.
Results may differ from a plain program's by a relative error of at most 0.012.
Values may be sent and summed in bfloat16 or wider, within the bound.
A program may use at most 64 MiB of HBM per device.

v0:
```python
import math

import jax
import jax.numpy as jnp
from jax import lax
from jax.sharding import PartitionSpec as P

RF1 = 64
RF2 = 128
TAPS = 16
NTAB = 64
GUARD = 16
HALO = 16


PRECISE = lax.Precision.HIGH


def dft_table(length, orient):
    counter = jnp.arange(length, dtype=jnp.int32)
    phase = counter[:, None] * counter[None, :] % length
    angle = 2.0 * math.pi / length * phase.astype(jnp.float32)
    return (jnp.cos(angle), orient * jnp.sin(angle))


def twiddle_table(lead_size, tail_size, orient):
    lead_idx = jnp.arange(lead_size, dtype=jnp.int32)
    tail_idx = jnp.arange(tail_size, dtype=jnp.int32)
    phase = lead_idx[:, None] * tail_idx[None, :] % (lead_size * tail_size)
    angle = 2.0 * math.pi / (lead_size * tail_size) * phase.astype(jnp.float32)
    return (jnp.cos(angle), orient * jnp.sin(angle))


def split_table(table):
    upper = table.astype(jnp.bfloat16)
    lower = (table - upper.astype(jnp.float32)).astype(jnp.bfloat16)
    return (upper, lower)


def lead_product(table, data):
    if data.dtype == jnp.bfloat16:
        upper, lower = split_table(table)
        first = jnp.einsum("ka,rab->rkb", upper, data, preferred_element_type=jnp.float32)
        return first + jnp.einsum("ka,rab->rkb", lower, data, preferred_element_type=jnp.float32)
    return jnp.einsum("ka,rab->rkb", table, data, precision=PRECISE)


def along_last(real_part, imag_part, lead_size, tail_size, orient, factor):
    height = real_part.shape[0]
    real_in = real_part.reshape(height, lead_size, tail_size)
    imag_in = imag_part.reshape(height, lead_size, tail_size)
    lead_cos, lead_sin = dft_table(lead_size, orient)
    step_real = lead_product(lead_cos, real_in) - lead_product(lead_sin, imag_in)
    step_imag = lead_product(lead_cos, imag_in) + lead_product(lead_sin, real_in)
    twist_cos, twist_sin = twiddle_table(lead_size, tail_size, orient)
    turned_real = step_real * twist_cos[None] - step_imag * twist_sin[None]
    turned_imag = step_real * twist_sin[None] + step_imag * twist_cos[None]
    tail_cos, tail_sin = dft_table(tail_size, orient)
    out_real = jnp.einsum("rkb,bm->rmk", turned_real, tail_cos, precision=PRECISE) - jnp.einsum(
        "rkb,bm->rmk", turned_imag, tail_sin, precision=PRECISE
    )
    out_imag = jnp.einsum("rkb,bm->rmk", turned_real, tail_sin, precision=PRECISE) + jnp.einsum(
        "rkb,bm->rmk", turned_imag, tail_cos, precision=PRECISE
    )
    return (factor * out_real.reshape(height, -1), factor * out_imag.reshape(height, -1))


def along_first(real_part, imag_part, lead_size, tail_size, orient, factor):
    columns = real_part.shape[1]
    real_in = real_part.reshape(lead_size, tail_size, columns)
    imag_in = imag_part.reshape(lead_size, tail_size, columns)
    lead_cos, lead_sin = dft_table(lead_size, orient)
    step_real = jnp.einsum("ka,abs->kbs", lead_cos, real_in, precision=PRECISE) - jnp.einsum(
        "ka,abs->kbs", lead_sin, imag_in, precision=PRECISE
    )
    step_imag = jnp.einsum("ka,abs->kbs", lead_cos, imag_in, precision=PRECISE) + jnp.einsum(
        "ka,abs->kbs", lead_sin, real_in, precision=PRECISE
    )
    twist_cos, twist_sin = twiddle_table(lead_size, tail_size, orient)
    turned_real = step_real * twist_cos[:, :, None] - step_imag * twist_sin[:, :, None]
    turned_imag = step_real * twist_sin[:, :, None] + step_imag * twist_cos[:, :, None]
    tail_cos, tail_sin = dft_table(tail_size, orient)
    out_real = jnp.einsum("kbs,bm->mks", turned_real, tail_cos, precision=PRECISE) - jnp.einsum(
        "kbs,bm->mks", turned_imag, tail_sin, precision=PRECISE
    )
    out_imag = jnp.einsum("kbs,bm->mks", turned_real, tail_sin, precision=PRECISE) + jnp.einsum(
        "kbs,bm->mks", turned_imag, tail_cos, precision=PRECISE
    )
    return (factor * out_real.reshape(-1, columns), factor * out_imag.reshape(-1, columns))


def whiten(spec_real, spec_imag):
    inverse = lax.rsqrt(jnp.maximum(spec_real * spec_real + spec_imag * spec_imag, 1.0))
    return ((spec_real * inverse).astype(jnp.bfloat16), (-spec_imag * inverse).astype(jnp.bfloat16))


def band_product(frame, band_upper, band_lower):
    first = jnp.dot(frame, band_upper, preferred_element_type=jnp.float32)
    return first + jnp.dot(frame, band_lower, preferred_element_type=jnp.float32)


def shards(signal, tap_table, range_shift, tap_index, ref_channel):
    source_id = ref_channel[0]
    is_source = lax.axis_index("chan") == source_id
    own_data = signal[0]
    pul_dev = own_data.shape[1]
    samples_len = own_data.shape[2]
    slab_len = range_shift.shape[0]
    az_count = lax.axis_size("az")
    lag_count = slab_len * az_count
    factor_range = 1.0 / math.sqrt(samples_len)
    spec_real, spec_imag = along_last(own_data[0], own_data[1], RF1, RF2, -1.0, factor_range)
    masked_data = jnp.where(is_source, own_data, jnp.zeros_like(own_data))
    ref_data = lax.psum(masked_data, "chan").astype(jnp.float32).astype(jnp.bfloat16)
    ref_real, ref_imag = along_last(ref_data[0], ref_data[1], RF1, RF2, -1.0, factor_range)
    filter_low_real, filter_low_imag = whiten(ref_real, ref_imag)
    filter_real = filter_low_real.astype(jnp.float32)
    filter_imag = filter_low_imag.astype(jnp.float32)
    prod_real = spec_real * filter_real - spec_imag * filter_imag
    prod_imag = spec_real * filter_imag + spec_imag * filter_real
    lag_real, lag_imag = along_last(prod_real, prod_imag, RF1, RF2, 1.0, factor_range)
    compressed = jnp.stack(
        [lag_real[:, GUARD : GUARD + lag_count], lag_imag[:, GUARD : GUARD + lag_count]]
    ).astype(jnp.bfloat16)
    padded = jnp.pad(compressed, ((0, 0), (0, 0), (HALO, slab_len + HALO)))
    main_part = padded[:, :, :lag_count].reshape(2, pul_dev, az_count, slab_len)
    after_part = padded[:, :, slab_len : slab_len + lag_count].reshape(
        2, pul_dev, az_count, slab_len
    )[..., : 2 * HALO]
    widened = jnp.concatenate([main_part, after_part], axis=3).reshape(
        2, pul_dev, az_count * (slab_len + 2 * HALO)
    )
    framed = lax.all_to_all(widened, "az", split_axis=2, concat_axis=1, tiled=True)
    chooser = (tap_index[:, None] == jnp.arange(NTAB, dtype=jnp.int32)[None, :]).astype(jnp.float32)
    tap_rows = jnp.dot(chooser, tap_table, precision=lax.Precision.HIGHEST)
    source_pos = jnp.arange(slab_len + 2 * HALO, dtype=jnp.int32)[:, None, None]
    target_pos = (
        jnp.arange(slab_len, dtype=jnp.int32)[None, :, None]
        + HALO
        + range_shift[None, :, None]
        + jnp.arange(TAPS, dtype=jnp.int32)[None, None, :]
        - TAPS // 2
    )
    banded = jnp.sum(jnp.where(source_pos == target_pos, tap_rows[None], 0.0), axis=2)
    band_upper, band_lower = split_table(banded)
    aligned_real = band_product(framed[0], band_upper, band_lower)
    aligned_imag = band_product(framed[1], band_upper, band_lower)
    pulse_total = aligned_real.shape[0]
    doppler_real, doppler_imag = along_first(
        aligned_real, aligned_imag, az_count, pul_dev, -1.0, 1.0 / math.sqrt(pulse_total)
    )
    return jnp.stack([doppler_real, doppler_imag])[None]


def solution(mesh):
    return jax.shard_map(
        shards,
        mesh=mesh,
        in_specs=(P("chan", None, "az", None), P(), P("az"), P("az"), P("az")),
        out_specs=P("chan", None, None, "az"),
        check_vma=False,
    )
```

profile of v0, /device:TPU:0, one launch (start us, length us, event | category | flops | bytes accessed | tf_op | source)
XLA Modules:
  0.0 95.3 jit_solution(10513515113329657731)
XLA Ops:
  7.3 1.9 %select_bitcast_fusion = bf16[2,16,8192]{2,1,0:T(8,128)(2,1)} fusion(bf16[1,2,16,8192]{3,2,1,0:T(8,128)(2,1)} %param.5, pred[]{:T(512)S(6)} %eq.47), kind=kLoop, calls=%fused_computation.68 | loop fusion | flops 262144 | bytes 1048577 | tf_op jit(solution)/shard_map/jit(_where)/select_n | solution.py:113
  10.4 0.3 fusion.118
  10.8 0.3 convolution_add_fusion.6
  11.1 0.3 convolution_add_fusion.4
  11.4 0.3 fusion.11
  11.8 0.3 fusion.12
  12.1 0.6 fusion.29
  12.7 0.6 fusion.27
  13.5 0.6 fusion.10
  14.1 0.6 fusion.5
  14.9 0.3 copy.75
  15.4 0.3 copy.78
  16.0 0.4 copy-done.5
  16.6 29.3 %all-reduce.3.cloned.1.call-done = bf16[2,16,8192]{2,1,0:T(8,128)(2,1)} async-done(((bf16[2,16,8192]{2,1,0:T(8,128)(2,1)}), bf16[2,16,8192]{2,1,0:T(8,128)(2,1)}) %all-reduce.3.cloned.1.call-update) | async-done | bytes 524304 | tf_op jit(solution)/shard_map/psum | solution.py:114
  45.9 1.1 %slice_bitcast_fusion = (bf16[2,8,64,128]{3,1,2,0:T(8,128)(2,1)S(1)}, bf16[2,8,64,128]{3,1,2,0:T(8,128)(2,1)S(1)}) fusion(bf16[2,16,8192]{2,1,0:T(8,128)(2,1)} %all-reduce.3.cloned.1.call-done), kind=kLoop, calls=%fused_computation.71 | loop fusion | bytes 1048576
  48.4 0.3 convolution_add_fusion.2
  48.7 0.3 convolution_add_fusion
  49.0 0.3 fusion.14
  49.4 0.3 fusion.16
  49.7 0.6 fusion.32
  50.3 1.4 %fusion.33 = f32[128,16,64]{0,2,1:T(8,128)} fusion(f32[16,64,128]{2,1,0:T(8,128)S(1)} %fusion.16, f32[16,64,128]{2,1,0:T(8,128)S(1)} %fusion.14, f32[64,128]{1,0:T(8,128)S(1)} %get-tuple-element.19, f32[64,128]{1,0:T(8,128)S(1)} %get-tuple-element.20), kind=kOutput, calls=%fused_computation.79 | convolution fusion | flops 101285888 | bytes 1638400 | tf_op jit(solution)/shard_map/rkb,bm->rmk/dot_general | solution.py:59
  51.7 1.6 %negate_bitcast_fusion = (f32[16,128,64]{1,2,0:T(8,128)}, f32[16,128,64]{1,2,0:T(8,128)}) fusion(f32[128,16,64]{0,2,1:T(8,128)S(1)} %fusion.32, f32[16,64,128]{2,1,0:T(8,128)S(1)} %fusion.16, f32[16,64,128]{2,1,0:T(8,128)S(1)} %fusion.14, f32[64,128]{1,0:T(8,128)S(1)} %get-tuple-element.19, f32[64,128]{1,0:T(8,128)S(1)} %get-tuple-element.20), kind=kOutput, calls=%fused_computation.62 | convolution fusion | flops 101810176 | bytes 2686976 | tf_op jit(solution)/shard_map/rkb,bm->rmk/dot_general | solution.py:62
  53.3 1.4 %copy.77 = f32[16,128,64]{2,1,0:T(8,128)S(1)} copy(f32[16,128,64]{1,2,0:T(8,128)} %get-tuple-element.8) | data formatting | bytes 1048576 | tf_op jit(solution)/shard_map/mul | solution.py:93
  54.7 1.0 %mul.962 = f32[16,64,128]{2,1,0:T(8,128)} reshape(f32[16,128,64]{2,1,0:T(8,128)S(1)} %copy.77) | data formatting | bytes 1048576 | tf_op jit(solution)/shard_map/mul | solution.py:93
  55.7 1.4 %copy.79 = f32[16,128,64]{2,1,0:T(8,128)S(1)} copy(f32[16,128,64]{1,2,0:T(8,128)} %get-tuple-element.7) | data formatting | bytes 1048576 | tf_op jit(solution)/shard_map/neg | solution.py:94
  57.1 1.0 %neg.13 = f32[16,64,128]{2,1,0:T(8,128)} reshape(f32[16,128,64]{2,1,0:T(8,128)S(1)} %copy.79) | data formatting | bytes 1048576 | tf_op jit(solution)/shard_map/neg | solution.py:94
  58.1 1.7 %fusion.8 = f32[16,128,64]{1,2,0:T(8,128)S(1)} fusion(f32[128,16,64]{0,2,1:T(8,128)} %fusion.33, f32[16,64,128]{2,1,0:T(8,128)S(1)} %fusion.16, f32[16,64,128]{2,1,0:T(8,128)S(1)} %fusion.14, f32[64,128]{1,0:T(8,128)S(1)} %get-tuple-element.19, f32[64,128]{1,0:T(8,128)S(1)} %get-tuple-element.20), kind=kOutput, calls=%fused_computation.25 | convolution fusion | flops 101564416 | bytes 2162688 | tf_op jit(solution)/shard_map/rkb,bm->rmk/dot_general | solution.py:59
  59.8 0.3 copy.76
  60.2 1.0 %mul.957 = f32[16,64,128]{2,1,0:T(8,128)} reshape(f32[16,128,64]{2,1,0:T(8,128)S(1)} %copy.76) | data formatting | bytes 1048576 | tf_op jit(solution)/shard_map/mul | solution.py:65
  61.2 0.3 copy-done.3
  61.5 1.2 %multiply_convert_fusion = (bf16[16,64,128]{2,1,0:T(8,128)(2,1)S(1)}, bf16[16,64,128]{2,1,0:T(8,128)(2,1)S(1)}) fusion(f32[16,64,128]{2,1,0:T(8,128)S(1)} %copy-done.3, f32[16,64,128]{2,1,0:T(8,128)S(1)} %copy-done.2, f32[16,64,128]{2,1,0:T(8,128)} %mul.957), kind=kLoop, calls=%fused_computation.61 | loop fusion | flops 917504 | bytes 2097152 | tf_op jit(solution)/shard_map/convert_element_type | solution.py:94
  62.8 0.7 fusion.84
  63.5 0.5 fusion.82
  64.1 0.5 fusion.3
  64.6 0.5 fusion.2
  65.2 0.6 fusion.35
  65.8 0.6 fusion.34
  66.4 0.6 fusion.20
  67.3 0.5 mul.979
  67.9 0.6 fusion.19
  68.8 0.5 mul.982
  69.6 0.7 copy.82
  70.3 1.3 %reshape.214 = bf16[8,2,2560]{2,1,0:T(2,128)(2,1)} reshape(bf16[1280,2,16]{2,1,0:T(2,128)(2,1)S(1)} %bitcast.209) | data formatting | bytes 163840
  71.6 5.5 %all-to-all-start = ((bf16[8,2,2560]{2,1,0:T(2,128)(2,1)}), bf16[8,2,2560]{2,1,0:T(2,128)(2,1)S(1)}, u32[]{:S(2)}, u32[]{:S(2)}) async-start(bf16[8,2,2560]{2,1,0:T(2,128)(2,1)} %reshape.214), calls=%async_computation | async-start | bytes 163840 | tf_op jit(solution)/shard_map/all_to_all | solution.py:133
  77.5 6.7 %all-to-all-done = bf16[8,2,2560]{2,1,0:T(2,128)(2,1)S(1)} async-done(((bf16[8,2,2560]{2,1,0:T(2,128)(2,1)}), bf16[8,2,2560]{2,1,0:T(2,128)(2,1)S(1)}, u32[]{:S(2)}, u32[]{:S(2)}) %all-to-all-start) | async-done | bytes 81952 | tf_op jit(solution)/shard_map/all_to_all | solution.py:133
  84.2 0.5 reshape.215
  84.6 0.6 copy.96
  87.8 0.7 maximum_bitcast_fusion
  (59 shorter events, 7.1 us)
Async XLA Ops:
  6.5 9.5 %copy-start = (f32[64,16]{0,1:T(8,128)S(1)}, f32[64,16]{0,1:T(8,128)}, u32[]{:S(2)}) copy-start(f32[64,16]{0,1:T(8,128)} %param.6) | copy-start | bytes 12292
  6.5 2.8 %copy-start.1 = (bf16[1,2,16,8192]{3,2,1,0:T(8,128)(2,1)S(1)}, bf16[1,2,16,8192]{3,2,1,0:T(8,128)(2,1)}, u32[]{:S(2)}) copy-start(bf16[1,2,16,8192]{3,2,1,0:T(8,128)(2,1)} %param.5) | copy-start | bytes 1572868
  6.5 39.3 %all-reduce.3.cloned.1.call-start = ((), (), s32[]{:S(2)}) async-start(), calls=%async_computation.1 | async-start | bytes 1048576 | tf_op jit(solution)/shard_map/psum | solution.py:114
  14.1 0.7 copy-start.4
  15.8 0.7 copy-start.5
  60.1 1.0 %copy-start.2 = (f32[16,64,128]{2,1,0:T(8,128)S(1)}, f32[16,64,128]{2,1,0:T(8,128)}, u32[]{:S(2)}) copy-start(f32[16,64,128]{2,1,0:T(8,128)} %mul.962) | copy-start | bytes 1572868
  60.1 1.4 %copy-start.3 = (f32[16,64,128]{2,1,0:T(8,128)S(1)}, f32[16,64,128]{2,1,0:T(8,128)}, u32[]{:S(2)}) copy-start(f32[16,64,128]{2,1,0:T(8,128)} %neg.13) | copy-start | bytes 1572868
  71.6 12.5 %all-to-all-start = ((bf16[8,2,2560]{2,1,0:T(2,128)(2,1)}), bf16[8,2,2560]{2,1,0:T(2,128)(2,1)S(1)}, u32[]{:S(2)}, u32[]{:S(2)}) async-start(bf16[8,2,2560]{2,1,0:T(2,128)(2,1)} %reshape.214), calls=%async_computation | async-start | bytes 163840 | tf_op jit(solution)/shard_map/all_to_all | solution.py:133
Sparse Core Ops, SparseCore 0:
  9.7 36.1 all-reduce.2
where the time goes:
time: 95.7 us; the launch traced here: 95.3 us
  waiting for transfers between devices  36 us (38%)
  matrix products  20.2 us (21%)
  between operations  14.7 us (15%)
  local copies, waits for them, and re-layouts  14.3 us (15%)
  starting transfers between devices  5.52 us (6%)
  other arithmetic  4.59 us (5%)
    psum x1, waiting for transfers between devices, shards(): lax.psum(masked_data, 'chan').astype(jnp.float32).astype(jnp.bfloat16)  29.3 us
    all_to_all x1, waiting for transfers between devices, shards(): lax.all_to_all(widened, 'az', split_axis=2, concat_axis=1, tiled=True)  6.7 us
    all_to_all x1, starting transfers between devices, shards(): lax.all_to_all(widened, 'az', split_axis=2, concat_axis=1, tiled=True)  5.52 us
    unnamed x22, local copies, waits for them, and re-layouts  3.93 us
    dot_general x3, matrix products, along_last(): jnp.einsum('rkb,bm->rmk', turned_imag, tail_sin, precision=PRECISE)  2.91 us
    dot_general x3, matrix products, along_last(): jnp.einsum('rkb,bm->rmk', turned_imag, tail_cos, precision=PRECISE)  2.87 us
    mul x6, local copies, waits for them, and re-layouts, along_last(): factor * out_real.reshape(height, -1)  2.63 us
    dot_general x3, matrix products, along_last(): jnp.einsum('rkb,bm->rmk', turned_real, tail_cos, precision=PRECISE)  2.63 us
  transfers between devices with their start and end apart: 2, of which 2 were waited for; matrix products, arithmetic and copies ran while one was open for 7% of the time, Pallas kernels for 0%

commit v1 on v0

v1 whole, which is shorter than its diff:
```python
import functools
import math

import jax
import jax.numpy as jnp
import numpy as np
from jax import lax
from jax.experimental import pallas as pl
from jax.experimental.pallas import tpu as pltpu
from jax.sharding import PartitionSpec as P

TAIL = 128
GUARD = 16
HALO = 16
MESH = pl.DeviceIdType.MESH


def complex_block(table, left):
    top, low = (-table.imag, table.imag) if left else (table.imag, -table.imag)
    return np.block([[table.real, top], [low, table.real]])


def tables(lead, lags, pulses, pul_dev):
    total = lead * TAIL
    lead_idx, tail_idx = np.arange(lead), np.arange(TAIL)
    rows = lags // TAIL + 1
    fwd_lead = complex_block(np.exp(-2j * np.pi * np.outer(lead_idx, lead_idx) / lead), True)
    fwd_tail = complex_block(np.exp(-2j * np.pi * np.outer(tail_idx, tail_idx) / TAIL), False)
    inv_tail = complex_block(np.exp(2j * np.pi * np.outer(tail_idx, tail_idx) / TAIL), False)
    inv_lead = complex_block(np.exp(2j * np.pi * np.outer(np.arange(rows), lead_idx) / lead), True)
    inv_lead = inv_lead.reshape(2, rows, -1).transpose(1, 0, 2).reshape(2 * rows, -1)
    twist = np.exp(-2j * np.pi * np.outer(lead_idx, tail_idx) / total) / math.sqrt(total)
    doppler = complex_block(np.exp(-2j * np.pi * np.outer(np.arange(pulses), np.arange(pulses)) / pulses), True)
    doppler = doppler.reshape(2 * pulses, 2, pulses).transpose(0, 2, 1).reshape(2 * pulses, 2 * pulses)
    low = [item.astype(jnp.bfloat16) for item in (fwd_lead, fwd_tail, inv_tail, inv_lead, doppler)]
    return low, np.stack([twist.real, twist.imag]).astype(np.float32)


def kernel(
    chan_count, az_count, sig, taps, shift, index, source, fwd_lead, fwd_tail, inv_tail, inv_lead, doppler, twist,
    out, quarter, spec, filt, packed, comp, framed, send_a, recv_a, send_b, recv_b, send_c, recv_c,
):
    me_chan, me_az = lax.axis_index("chan"), lax.axis_index("az")
    pul_dev = sig.shape[0]
    lead = sig.shape[1] // 2
    part = pul_dev // chan_count
    slab = shift.shape[1]
    rows = packed.shape[0]
    pulses = az_count * pul_dev

    barrier = pltpu.get_barrier_semaphore()
    for step in range(1, chan_count):
        pl.semaphore_signal(
            barrier, inc=1, device_id={"chan": lax.rem(me_chan + step, chan_count)}, device_id_type=MESH
        )
    for step in range(1, az_count):
        pl.semaphore_signal(barrier, inc=1, device_id={"az": lax.rem(me_az + step, az_count)}, device_id_type=MESH)
    pl.semaphore_wait(barrier, chan_count + az_count - 2)

    first = []
    for step in [*range(2, chan_count), 1]:
        to = lax.rem(me_chan + step, chan_count)
        first.append(
            pltpu.make_async_remote_copy(
                src_ref=sig.at[pl.ds(to * part, part)],
                dst_ref=quarter.at[me_chan],
                send_sem=send_a.at[step],
                recv_sem=recv_a.at[step],
                device_id={"chan": to},
                device_id_type=MESH,
            )
        )
        first[-1].start()
    quarter[me_chan] = sig[pl.ds(me_chan * part, part)]

    twist_real, twist_imag = twist[0], twist[1]

    def forward(blocks):
        data = jnp.concatenate(blocks, axis=1) if len(blocks) > 1 else blocks[0]
        step = jnp.dot(fwd_lead[...], data, preferred_element_type=jnp.float32)
        turned = []
        for pos in range(len(blocks)):
            real = step[:lead, pos * TAIL : (pos + 1) * TAIL]
            imag = step[lead:, pos * TAIL : (pos + 1) * TAIL]
            turned.append(
                jnp.concatenate(
                    [real * twist_real - imag * twist_imag, real * twist_imag + imag * twist_real], axis=1
                ).astype(jnp.bfloat16)
            )
        turned = jnp.concatenate(turned, axis=0) if len(turned) > 1 else turned[0]
        return jnp.dot(turned, fwd_tail[...], preferred_element_type=jnp.float32)

    spec[...] = forward([sig[pos] for pos in range(pul_dev)]).reshape(spec.shape)

    entries = taps.shape[0]
    chooser = (lax.broadcasted_iota(jnp.int32, (entries, slab), 0) == index[...]).astype(jnp.bfloat16)
    tap_rows = lax.dot_general(
        taps[...].astype(jnp.bfloat16), chooser, (((0,), (0,)), ((), ())), preferred_element_type=jnp.float32
    )
    tap_count = tap_rows.shape[0]
    reach = slab + TAIL
    offset = (
        lax.broadcasted_iota(jnp.int32, (reach, slab), 0)
        - lax.broadcasted_iota(jnp.int32, (reach, slab), 1)
        - (HALO - tap_count // 2)
        - shift[...]
    )
    band = jnp.zeros((reach, slab), jnp.float32)
    for tap in range(tap_count):
        band = jnp.where(offset == tap, tap_rows[tap : tap + 1, :], band)
    band = band.astype(jnp.bfloat16)

    for copy in first:
        copy.wait()
    chosen = quarter[source[0]]
    ref = forward([chosen[pos] for pos in range(part)])
    real, imag = ref[:, :TAIL], ref[:, TAIL:]
    inverse = lax.rsqrt(jnp.maximum(real * real + imag * imag, 1.0))
    filt[me_chan] = jnp.concatenate([real * inverse, -imag * inverse], axis=1).astype(jnp.bfloat16)

    second = []
    for step in [*range(2, chan_count), 1]:
        to = lax.rem(me_chan + step, chan_count)
        second.append(
            pltpu.make_async_remote_copy(
                src_ref=filt.at[me_chan],
                dst_ref=filt.at[me_chan],
                send_sem=send_b.at[step],
                recv_sem=recv_b.at[step],
                device_id={"chan": to},
                device_id_type=MESH,
            )
        )
        second[-1].start()
    for copy in second:
        copy.wait()

    weight = filt[...].reshape(pul_dev * lead, 2 * TAIL).astype(jnp.float32)
    own = spec[...].reshape(pul_dev * lead, 2 * TAIL)
    spec_real, spec_imag = own[:, :TAIL], own[:, TAIL:]
    filt_real, filt_imag = weight[:, :TAIL], weight[:, TAIL:]
    product = jnp.concatenate(
        [spec_real * filt_real - spec_imag * filt_imag, spec_real * filt_imag + spec_imag * filt_real], axis=1
    ).astype(jnp.bfloat16)
    lagged = jnp.dot(product, inv_tail[...], preferred_element_type=jnp.float32)
    columns = []
    for pos in range(pul_dev):
        real = lagged[pos * lead : (pos + 1) * lead, :TAIL]
        imag = lagged[pos * lead : (pos + 1) * lead, TAIL:]
        columns.append(
            jnp.concatenate(
                [real * twist_real + imag * twist_imag, imag * twist_real - real * twist_imag], axis=0
            ).astype(jnp.bfloat16)
        )
    lags = jnp.dot(inv_lead[...], jnp.concatenate(columns, axis=1), preferred_element_type=jnp.float32)
    for pos in range(pul_dev):
        block = lags[:, pos * TAIL : (pos + 1) * TAIL]
        for row in range(rows):
            packed[row, 2 * pos : 2 * pos + 2, :] = block[2 * row : 2 * row + 2, :]
    when = lax.broadcasted_iota(jnp.int32, packed.shape, 0) * TAIL + lax.broadcasted_iota(jnp.int32, packed.shape, 2)
    inside = (when >= GUARD) & (when < GUARD + slab * az_count)
    comp[...] = jnp.where(inside, packed[...], 0.0).astype(jnp.bfloat16)

    third = []
    for step in range(1, az_count):
        to = lax.rem(me_az + step, az_count)
        third.append(
            pltpu.make_async_remote_copy(
                src_ref=comp.at[pl.ds(to, 2)],
                dst_ref=framed.at[me_az],
                send_sem=send_c.at[step],
                recv_sem=recv_c.at[step],
                device_id={"az": to},
                device_id_type=MESH,
            )
        )
        third[-1].start()
    framed[me_az] = comp[pl.ds(me_az, 2)]
    for copy in third:
        copy.wait()

    main = framed[:, 0].reshape(2 * pulses, TAIL)
    after = framed[:, 1].reshape(2 * pulses, TAIL)
    aligned = jnp.dot(jnp.concatenate([main, after], axis=1), band, preferred_element_type=jnp.float32)
    picture = jnp.dot(doppler[...], aligned.astype(jnp.bfloat16), preferred_element_type=jnp.float32)
    out[...] = picture * (1.0 / math.sqrt(pulses))


def shards(signal, tap_table, range_shift, tap_index, ref_channel):
    chan_count, az_count = lax.axis_size("chan"), lax.axis_size("az")
    pul_dev, samples = signal.shape[2], signal.shape[3]
    lead = samples // TAIL
    slab = range_shift.shape[0]
    part = pul_dev // chan_count
    pulses = pul_dev * az_count
    lags = slab * az_count
    rows = lags // TAIL + 1
    low, twist = tables(lead, lags, pulses, pul_dev)
    sig = signal[0].reshape(2, pul_dev, lead, TAIL).transpose(1, 0, 2, 3).reshape(pul_dev, 2 * lead, TAIL)
    vmem = pl.BlockSpec(memory_space=pltpu.VMEM)
    dma = pltpu.SemaphoreType.DMA
    picture = pl.pallas_call(
        functools.partial(kernel, chan_count, az_count),
        out_shape=jax.ShapeDtypeStruct((2 * pulses, slab), jnp.float32),
        in_specs=[vmem] * 4 + [pl.BlockSpec(memory_space=pltpu.SMEM)] + [vmem] * 6,
        out_specs=vmem,
        scratch_shapes=[
            pltpu.VMEM((chan_count, part, 2 * lead, TAIL), jnp.bfloat16),
            pltpu.VMEM((pul_dev, lead, 2 * TAIL), jnp.float32),
            pltpu.VMEM((chan_count, part * lead, 2 * TAIL), jnp.bfloat16),
            pltpu.VMEM((rows, 2 * pul_dev, TAIL), jnp.float32),
            pltpu.VMEM((rows, 2 * pul_dev, TAIL), jnp.bfloat16),
            pltpu.VMEM((az_count, 2, 2 * pul_dev, TAIL), jnp.bfloat16),
            dma((chan_count,)),
            dma((chan_count,)),
            dma((chan_count,)),
            dma((chan_count,)),
            dma((az_count,)),
            dma((az_count,)),
        ],
        compiler_params=pltpu.CompilerParams(collective_id=0, has_side_effects=True, vmem_limit_bytes=48 * 2**20),
    )(
        sig,
        tap_table,
        range_shift.reshape(1, slab),
        tap_index.reshape(1, slab),
        ref_channel,
        *[jnp.asarray(item) for item in low],
        jnp.asarray(twist),
    )
    return picture.reshape(1, 2, pulses, slab)


def solution(mesh):
    return jax.shard_map(
        shards,
        mesh=mesh,
        in_specs=(P("chan", None, "az", None), P(), P("az"), P("az"), P("az")),
        out_specs=P("chan", None, None, "az"),
        check_vma=False,
    )
```

time: 95.7 us -> 29.8 us (0.31)
  waiting for transfers between devices: 36 us -> 0 us
  Pallas kernels: 0 us -> 25.7 us
  matrix products: 20.2 us -> 0 us
  between operations: 14.7 us -> 0.79 us
  local copies, waits for them, and re-layouts: 14.3 us -> 3.15 us
  starting transfers between devices: 5.52 us -> 0 us
  other arithmetic: 4.59 us -> 0 us
    psum x1 -> x0, waiting for transfers between devices: 29.3 us -> none  [shards(): lax.psum(masked_data, 'chan').astype(jnp.float32).astype(jnp.bfloat16)]
    pallas_call x0 -> x1, Pallas kernels: none -> 25.7 us  [shards(): pl.pallas_call(functools.partial(kernel, chan_count, az_count), out_shape...]
    dot_general x45 -> x0, matrix products: 20.2 us -> none  [the longest x3 2.91 us: along_last(): jnp.einsum('rkb,bm->rmk', turned_imag, tail_sin, precision=PRECISE)]
    all_to_all x1 -> x0, waiting for transfers between devices: 6.7 us -> none  [shards(): lax.all_to_all(widened, 'az', split_axis=2, concat_axis=1, tiled=True)]
    mul x14 -> x0, local copies, waits for them, and re-layouts: 6.37 us -> none  [the longest x6 2.63 us: along_last(): factor * out_real.reshape(height, -1)]
    all_to_all x1 -> x0, starting transfers between devices: 5.52 us -> none  [shards(): lax.all_to_all(widened, 'az', split_axis=2, concat_axis=1, tiled=True)]
    neg x2 -> x0, local copies, waits for them, and re-layouts: 2.41 us -> none  [whiten(): -spec_imag * inverse]
    select_n x1 -> x0, other arithmetic: 1.89 us -> none  [shards(): masked_data = jnp.where(is_source, own_data, jnp.zeros_like(own_data))]
  transfers between devices with their start and end apart: 2 -> 0, of which waited for: 2 -> 0; matrix products, arithmetic and copies ran while one was open for 7% -> 0% of each run, Pallas kernels for 0% -> 0%
where the time goes in v1:
time: 29.8 us; the launch traced here: 29.6 us
  Pallas kernels  25.7 us (86%)
  local copies, waits for them, and re-layouts  3.15 us (11%)
  between operations  0.79 us (3%)
    pallas_call x1, Pallas kernels, shards(): pl.pallas_call(functools.partial(kernel, chan_count, az_count), out_shape...  25.7 us
    unnamed x21, local copies, waits for them, and re-layouts  3.12 us

profile of v1, /device:TPU:0, one launch (start us, length us, event | category | flops | bytes accessed | tf_op | source)
XLA Modules:
  0.0 29.6 jit_solution(6893780318636821650)
XLA Ops:
  0.0 1.2 %copy.14 = bf16[4,8,64,128]{3,2,1,0:T(8,128)(2,1)S(1)} copy(bf16[4,8,64,128]{3,1,2,0:T(8,128)(2,1)} %bitcast.16) | data formatting | bytes 1048576
  1.2 0.0 copy-start.8
  1.2 0.0 copy-start
  1.2 0.0 copy-start.1
  1.2 0.0 copy-start.2
  1.2 0.0 copy-start.3
  1.3 0.0 copy-start.4
  1.3 0.6 %copy-done.8 = f32[64,16]{0,1:T(8,128)S(1)} copy-done((f32[64,16]{0,1:T(8,128)S(1)}, f32[64,16]{0,1:T(8,128)}, u32[]{:S(2)}) %copy-start.8) | copy-done | bytes 4120
  1.9 0.0 copy-start.5
  1.9 0.1 copy.13.taps
  2.6 0.0 copy-start.6
  2.6 0.0 copy-start.7
  2.6 0.0 copy-done
  2.6 0.0 copy-done.1
  2.6 0.0 copy-done.2
  2.7 0.0 copy-done.3
  2.7 0.0 copy-done.4
  2.7 0.0 copy-done.5
  2.7 0.6 %copy-done.6 = s32[128]{0:T(128)S(1)} copy-done((s32[128]{0:T(128)S(1)}, s32[128]{0:T(128)}, u32[]{:S(2)}) %copy-start.6) | copy-done | bytes 536
  3.3 0.0 copy-done.7
  3.3 25.7 %shard_map.109 = f32[256,128]{1,0:T(8,128)S(1)} custom-call(bf16[16,128,128]{2,1,0:T(8,128)(2,1)S(1)} %bitcast.11, f32[64,16]{1,0:T(8,128)S(1)} %copy.13.taps, s32[1,128]{1,0:T(1,128)S(1)} %bitcast.13, s32[1,128]{1,0:T(1,128)S(1)} %bitcast.14, s32[1]{0:T(128)S(6)} %copy.16.source, bf16[128,128]{1,0:T(8,128)(2,1)S(1)} %copy-done.4, ...), custom_call_target="tpu_custom_call" | custom-call | tf_op jit(solution)/shard_map/pallas_call | solution.py:202
  29.0 0.7 %copy.17 = f32[1,2,128,128]{3,2,1,0:T(8,128)} copy(f32[1,2,128,128]{3,2,1,0:T(8,128)S(1)} %bitcast.12) | data formatting | bytes 262144
  (1 shorter events, 0.0 us)
Async XLA Ops:
  1.2 0.7 %copy-start.8 = (f32[64,16]{0,1:T(8,128)S(1)}, f32[64,16]{0,1:T(8,128)}, u32[]{:S(2)}) copy-start(f32[64,16]{0,1:T(8,128)} %param.12) | copy-start | bytes 12292
  1.2 1.5 %copy-start = (bf16[256,256]{1,0:T(8,128)(2,1)S(1)}, bf16[256,256]{1,0:T(8,128)(2,1)}, u32[]{:S(2)}) copy-start(bf16[256,256]{1,0:T(8,128)(2,1)} %constant.13.clone.fwd_tail) | copy-start | bytes 393220
  1.2 1.5 %copy-start.1 = (bf16[256,256]{1,0:T(8,128)(2,1)S(1)}, bf16[256,256]{1,0:T(8,128)(2,1)}, u32[]{:S(2)}) copy-start(bf16[256,256]{1,0:T(8,128)(2,1)} %constant.14.clone.inv_tail) | copy-start | bytes 393220
  1.2 1.4 %copy-start.2 = (bf16[256,256]{1,0:T(8,128)(2,1)S(1)}, bf16[256,256]{1,0:T(8,128)(2,1)}, u32[]{:S(2)}) copy-start(bf16[256,256]{1,0:T(8,128)(2,1)} %constant.16.clone.doppler) | copy-start | bytes 393220
  1.2 1.4 %copy-start.3 = (f32[2,64,128]{2,1,0:T(8,128)S(1)}, f32[2,64,128]{2,1,0:T(8,128)}, u32[]{:S(2)}) copy-start(f32[2,64,128]{2,1,0:T(8,128)} %constant.17.clone.twist) | copy-start | bytes 196612
  1.3 1.4 %copy-start.4 = (bf16[128,128]{1,0:T(8,128)(2,1)S(1)}, bf16[128,128]{1,0:T(8,128)(2,1)}, u32[]{:S(2)}) copy-start(bf16[128,128]{1,0:T(8,128)(2,1)} %constant.12.clone.fwd_lead) | copy-start | bytes 98308
  1.9 0.8 %copy-start.5 = (bf16[18,128]{1,0:T(8,128)(2,1)S(1)}, bf16[18,128]{1,0:T(8,128)(2,1)}, u32[]{:S(2)}) copy-start(bf16[18,128]{1,0:T(8,128)(2,1)} %constant.15.clone.inv_lead) | copy-start | bytes 13828
  2.6 0.7 %copy-start.6 = (s32[128]{0:T(128)S(1)}, s32[128]{0:T(128)}, u32[]{:S(2)}) copy-start(s32[128]{0:T(128)} %param.13) | copy-start | bytes 1540
  2.6 0.7 %copy-start.7 = (s32[128]{0:T(128)S(1)}, s32[128]{0:T(128)}, u32[]{:S(2)}) copy-start(s32[128]{0:T(128)} %param.14) | copy-start | bytes 1540

commit v2 on v1

v2 whole, which is shorter than its diff:
```python
import functools
import math

import jax
import jax.numpy as jnp
import numpy as np
from jax import lax
from jax.experimental import pallas as pl
from jax.experimental.pallas import tpu as pltpu
from jax.sharding import PartitionSpec as P

TAIL = 128
GUARD = 16
HALO = 16
MESH = pl.DeviceIdType.MESH


def complex_block(table, left):
    top, low = (-table.imag, table.imag) if left else (table.imag, -table.imag)
    return np.block([[table.real, top], [low, table.real]])


def tables(lead, lags, az_count, pul_dev, chunks, groups):
    total = lead * TAIL
    pulses = az_count * pul_dev
    lead_idx, tail_idx = np.arange(lead), np.arange(TAIL)
    rows = lags // TAIL + 1
    fwd_lead = complex_block(np.exp(-2j * np.pi * np.outer(lead_idx, lead_idx) / lead), True)
    fwd_tail = complex_block(np.exp(-2j * np.pi * np.outer(tail_idx, tail_idx) / TAIL), False)
    inv_tail = complex_block(np.exp(2j * np.pi * np.outer(tail_idx, tail_idx) / TAIL), False)
    inv_lead = complex_block(np.exp(2j * np.pi * np.outer(np.arange(rows), lead_idx) / lead), True)
    inv_lead = inv_lead.reshape(2, rows, -1).transpose(1, 0, 2).reshape(2 * rows, -1)
    twist = np.exp(-2j * np.pi * np.outer(lead_idx, tail_idx) / total) / math.sqrt(total)
    doppler = complex_block(np.exp(-2j * np.pi * np.outer(np.arange(pulses), np.arange(pulses)) / pulses), True)
    doppler = doppler.reshape(2 * pulses, 2, az_count, 2, groups, -1).transpose(0, 4, 2, 3, 5, 1)
    low = [fwd_lead, fwd_tail, inv_tail, inv_lead, doppler.reshape(2 * pulses, 2 * pulses)]
    return [item.astype(jnp.bfloat16) for item in low], np.stack([twist.real, twist.imag]).astype(np.float32)


def kernel(
    chan_count, az_count, chunks, groups, sig, taps, shift, index, source, fwd_lead, fwd_tail, inv_tail, inv_lead,
    doppler, twist, out, mate, cand, spec, filt, packed, comp, framed, send_a, recv_a, send_b, recv_b, send_c, recv_c,
    send_d, recv_d,
):
    me_chan, me_az = lax.axis_index("chan"), lax.axis_index("az")
    pul_dev, lead = sig.shape[1], sig.shape[2]
    half = pul_dev // 2
    part = half // chunks
    chips = chan_count // 2
    side, chip = lax.rem(me_chan, 2), me_chan // 2
    other = 1 - side
    sibling = {"chan": chip * 2 + other}
    slab = shift.shape[1]
    rows = comp.shape[1]
    per_group = chunks // groups

    def across(step):
        return {"chan": lax.rem(chip + step, chips) * 2 + side}

    def along(step):
        return lax.rem(me_az + step, az_count)

    barrier = pltpu.get_barrier_semaphore()
    peers = [sibling, *[across(step) for step in range(1, chips)], *[{"az": along(step)} for step in range(1, az_count)]]
    for peer in peers:
        pl.semaphore_signal(barrier, inc=1, device_id=peer, device_id_type=MESH)
    pl.semaphore_wait(barrier, len(peers))

    started = []

    def send(src, dst, send_sem, recv_sem, peer):
        copy = pltpu.make_async_remote_copy(
            src_ref=src, dst_ref=dst, send_sem=send_sem, recv_sem=recv_sem, device_id=peer, device_id_type=MESH
        )
        copy.start()
        started.append(copy)
        return copy

    first = [
        send(sig.at[:, pl.ds(other * half + pos * part, part)], mate.at[pos], send_a.at[pos], recv_a.at[pos], sibling)
        for pos in range(chunks)
    ]
    chosen_side, chosen_chip = lax.rem(source[0], 2), source[0] // 2
    second = []
    for pos in range(chunks):
        first[pos].wait_recv()
        mine = sig[:, pl.ds(side * half + pos * part, part)]
        cand[chip, pos] = jnp.where(chosen_side == side, mine, mate[pos])
        second.append(
            [
                send(
                    cand.at[chip, pos], cand.at[chip, pos], send_b.at[step, pos], recv_b.at[step, pos], across(step)
                )
                for step in range(1, chips)
            ]
        )

    twist_real, twist_imag = twist[0], twist[1]

    def forward(blocks):
        step = jnp.dot(fwd_lead[...], jnp.concatenate(blocks, axis=1), preferred_element_type=jnp.float32)
        turned = []
        for pos in range(len(blocks)):
            real = step[:lead, pos * TAIL : (pos + 1) * TAIL]
            imag = step[lead:, pos * TAIL : (pos + 1) * TAIL]
            turned.append(
                jnp.concatenate(
                    [real * twist_real - imag * twist_imag, real * twist_imag + imag * twist_real], axis=1
                ).astype(jnp.bfloat16)
            )
        return jnp.dot(jnp.concatenate(turned, axis=0), fwd_tail[...], preferred_element_type=jnp.float32)

    def stacked(block):
        return [jnp.concatenate([block[0, pos], block[1, pos]], axis=0) for pos in range(block.shape[1])]

    spec[...] = forward(stacked(sig[...])).reshape(spec.shape)

    entries = taps.shape[0]
    chooser = (lax.broadcasted_iota(jnp.int32, (entries, slab), 0) == index[...]).astype(jnp.bfloat16)
    tap_rows = lax.dot_general(
        taps[...].astype(jnp.bfloat16), chooser, (((0,), (0,)), ((), ())), preferred_element_type=jnp.float32
    )
    tap_count = tap_rows.shape[0]
    reach = slab + TAIL
    offset = (
        lax.broadcasted_iota(jnp.int32, (reach, slab), 0)
        - lax.broadcasted_iota(jnp.int32, (reach, slab), 1)
        - (HALO - tap_count // 2)
        - shift[...]
    )
    band = jnp.zeros((reach, slab), jnp.float32)
    for tap in range(tap_count):
        band = jnp.where(offset == tap, tap_rows[tap : tap + 1, :], band)
    band = band.astype(jnp.bfloat16)

    def backward(which, pos):
        weight = filt[which, pos].astype(jnp.float32)
        own = spec[which, pos]
        spec_real, spec_imag = own[:, :TAIL], own[:, TAIL:]
        filt_real, filt_imag = weight[:, :TAIL], weight[:, TAIL:]
        product = jnp.concatenate(
            [spec_real * filt_real - spec_imag * filt_imag, spec_real * filt_imag + spec_imag * filt_real], axis=1
        ).astype(jnp.bfloat16)
        lagged = jnp.dot(product, inv_tail[...], preferred_element_type=jnp.float32)
        columns = []
        for step in range(part):
            real = lagged[step * lead : (step + 1) * lead, :TAIL]
            imag = lagged[step * lead : (step + 1) * lead, TAIL:]
            columns.append(
                jnp.concatenate(
                    [real * twist_real + imag * twist_imag, imag * twist_real - real * twist_imag], axis=0
                ).astype(jnp.bfloat16)
            )
        lags = jnp.dot(inv_lead[...], jnp.concatenate(columns, axis=1), preferred_element_type=jnp.float32)
        group, place = pos // per_group, pos % per_group
        for step in range(part):
            start = 2 * (place * part + step)
            for row in range(rows):
                packed[which, group, row, start : start + 2, :] = lags[
                    2 * row : 2 * row + 2, step * TAIL : (step + 1) * TAIL
                ]

    fourth = []
    for pos in range(chunks):
        for copy in second[pos]:
            copy.wait_recv()
        chosen = cand[0, pos]
        for place in range(1, chips):
            chosen = jnp.where(chosen_chip == place, cand[place, pos], chosen)
        ref = forward(stacked(chosen))
        real, imag = ref[:, :TAIL], ref[:, TAIL:]
        inverse = lax.rsqrt(jnp.maximum(real * real + imag * imag, 1.0))
        filt[side, pos] = jnp.concatenate([real * inverse, -imag * inverse], axis=1).astype(jnp.bfloat16)
        third = send(filt.at[side, pos], filt.at[side, pos], send_c.at[pos], recv_c.at[pos], sibling)
        backward(side, pos)
        third.wait_recv()
        backward(other, pos)
        if pos % per_group == per_group - 1:
            group = pos // per_group
            lags = jnp.concatenate([packed[0, group], packed[1, group]], axis=1)
            when = lax.broadcasted_iota(jnp.int32, lags.shape, 0) * TAIL + lax.broadcasted_iota(
                jnp.int32, lags.shape, 2
            )
            inside = (when >= GUARD) & (when < GUARD + slab * az_count)
            comp[group] = jnp.where(inside, lags, 0.0).astype(jnp.bfloat16)
            fourth.append(
                [
                    send(
                        comp.at[group, pl.ds(along(step), 2)],
                        framed.at[group, me_az],
                        send_d.at[group, step],
                        recv_d.at[group, step],
                        {"az": along(step)},
                    )
                    for step in range(1, az_count)
                ]
            )
            framed[group, me_az] = comp[group, pl.ds(me_az, 2)]

    aligned = []
    for group in range(groups):
        for copy in fourth[group]:
            copy.wait_recv()
        main = framed[group, :, 0].reshape(az_count * comp.shape[2], TAIL)
        after = framed[group, :, 1].reshape(az_count * comp.shape[2], TAIL)
        aligned.append(
            jnp.dot(jnp.concatenate([main, after], axis=1), band, preferred_element_type=jnp.float32).astype(
                jnp.bfloat16
            )
        )
    picture = jnp.dot(doppler[...], jnp.concatenate(aligned, axis=0), preferred_element_type=jnp.float32)
    out[...] = picture * (1.0 / math.sqrt(az_count * pul_dev))
    for copy in started:
        copy.wait_send()


def shards(signal, tap_table, range_shift, tap_index, ref_channel):
    chan_count, az_count = lax.axis_size("chan"), lax.axis_size("az")
    pul_dev, samples = signal.shape[2], signal.shape[3]
    lead = samples // TAIL
    slab = range_shift.shape[0]
    chips = chan_count // 2
    chunks, groups = pul_dev // 4, 2
    part = pul_dev // 2 // chunks
    pulses = pul_dev * az_count
    lags = slab * az_count
    rows = lags // TAIL + 1
    low, twist = tables(lead, lags, az_count, pul_dev, chunks, groups)
    sig = signal[0].reshape(2, pul_dev, lead, TAIL)
    vmem = pl.BlockSpec(memory_space=pltpu.VMEM)
    dma = pltpu.SemaphoreType.DMA
    picture = pl.pallas_call(
        functools.partial(kernel, chan_count, az_count, chunks, groups),
        out_shape=jax.ShapeDtypeStruct((2 * pulses, slab), jnp.float32),
        in_specs=[vmem] * 4 + [pl.BlockSpec(memory_space=pltpu.SMEM)] + [vmem] * 6,
        out_specs=vmem,
        scratch_shapes=[
            pltpu.VMEM((chunks, 2, part, lead, TAIL), jnp.bfloat16),
            pltpu.VMEM((chips, chunks, 2, part, lead, TAIL), jnp.bfloat16),
            pltpu.VMEM((2, chunks, part * lead, 2 * TAIL), jnp.float32),
            pltpu.VMEM((2, chunks, part * lead, 2 * TAIL), jnp.bfloat16),
            pltpu.VMEM((2, groups, rows, pul_dev // groups, TAIL), jnp.float32),
            pltpu.VMEM((groups, rows, 2 * pul_dev // groups, TAIL), jnp.bfloat16),
            pltpu.VMEM((groups, az_count, 2, 2 * pul_dev // groups, TAIL), jnp.bfloat16),
            dma((chunks,)),
            dma((chunks,)),
            dma((chips, chunks)),
            dma((chips, chunks)),
            dma((chunks,)),
            dma((chunks,)),
            dma((groups, az_count)),
            dma((groups, az_count)),
        ],
        compiler_params=pltpu.CompilerParams(collective_id=0, has_side_effects=True, vmem_limit_bytes=48 * 2**20),
    )(
        sig,
        tap_table,
        range_shift.reshape(1, slab),
        tap_index.reshape(1, slab),
        ref_channel,
        *[jnp.asarray(item) for item in low],
        jnp.asarray(twist),
    )
    return picture.reshape(1, 2, pulses, slab)


def solution(mesh):
    return jax.shard_map(
        shards,
        mesh=mesh,
        in_specs=(P("chan", None, "az", None), P(), P("az"), P("az"), P("az")),
        out_specs=P("chan", None, None, "az"),
        check_vma=False,
    )
```

time: 29.8 us -> 25.3 us (0.85)
  Pallas kernels: 25.7 us -> 21 us
    pallas_call x1, Pallas kernels: 25.7 us -> 21 us  [shards(): pl.pallas_call(functools.partial(kernel, chan_count, az_count, chunks, gr...]
    unnamed x21 -> x19, local copies, waits for them, and re-layouts: 3.12 us -> 3.32 us
where the time goes in v2:
time: 25.3 us; the launch traced here: 25.1 us
  Pallas kernels  21 us (83%)
  local copies, waits for them, and re-layouts  3.32 us (13%)
  between operations  0.77 us (3%)
    pallas_call x1, Pallas kernels, shards(): pl.pallas_call(functools.partial(kernel, chan_count, az_count, chunks, gr...  21 us
    unnamed x19, local copies, waits for them, and re-layouts  3.32 us

profile of v2, /device:TPU:0, one launch (start us, length us, event | category | flops | bytes accessed | tf_op | source)
XLA Modules:
  0.0 25.1 jit_solution(2083849849037479518)
XLA Ops:
  0.7 0.8 %copy.12.taps = f32[64,16]{1,0:T(8,128)S(1)} copy(f32[64,16]{0,1:T(8,128)} %param.12) | data formatting | bytes 8192 | tf_op args[1]
  1.4 0.0 copy-start
  1.4 0.0 copy-start.1
  1.4 0.0 copy-start.2
  1.5 0.0 copy-start.3
  1.5 0.0 copy-start.4
  1.5 0.0 copy-start.5
  1.5 1.2 %copy.13 = bf16[4,8,64,128]{3,2,1,0:T(8,128)(2,1)S(1)} copy(bf16[4,8,64,128]{3,1,2,0:T(8,128)(2,1)} %bitcast.12) | data formatting | bytes 1048576
  2.8 0.0 copy-start.6
  2.8 0.0 copy-start.7
  2.8 0.0 copy-done
  2.8 0.0 copy-done.1
  2.8 0.0 copy-done.2
  2.8 0.0 copy-done.3
  2.8 0.0 copy-done.4
  2.8 0.0 copy-done.5
  2.8 0.6 %copy-done.6 = s32[128]{0:T(128)S(1)} copy-done((s32[128]{0:T(128)S(1)}, s32[128]{0:T(128)}, u32[]{:S(2)}) %copy-start.6) | copy-done | bytes 536
  3.4 0.0 copy-done.7
  3.4 21.0 %shard_map.109 = f32[256,128]{1,0:T(8,128)S(1)} custom-call(bf16[2,16,64,128]{3,2,1,0:T(8,128)(2,1)S(1)} %bitcast.8, f32[64,16]{1,0:T(8,128)S(1)} %copy.12.taps, s32[1,128]{1,0:T(1,128)S(1)} %bitcast.10, s32[1,128]{1,0:T(1,128)S(1)} %bitcast.11, s32[1]{0:T(128)S(6)} %copy.15.source, bf16[128,128]{1,0:T(8,128)(2,1)S(1)} %copy-done.4, ...), custom_call_target="tpu_custom_call" | custom-call | tf_op jit(solution)/shard_map/pallas_call | solution.py:232
  24.5 0.7 %copy.16 = f32[1,2,128,128]{3,2,1,0:T(8,128)} copy(f32[1,2,128,128]{3,2,1,0:T(8,128)S(1)} %bitcast.9) | data formatting | bytes 262144
Async XLA Ops:
  1.4 1.3 %copy-start = (bf16[256,256]{1,0:T(8,128)(2,1)S(1)}, bf16[256,256]{1,0:T(8,128)(2,1)}, u32[]{:S(2)}) copy-start(bf16[256,256]{1,0:T(8,128)(2,1)} %constant.16.clone.doppler) | copy-start | bytes 393220
  1.4 1.4 %copy-start.1 = (bf16[256,256]{1,0:T(8,128)(2,1)S(1)}, bf16[256,256]{1,0:T(8,128)(2,1)}, u32[]{:S(2)}) copy-start(bf16[256,256]{1,0:T(8,128)(2,1)} %constant.14.clone.inv_tail) | copy-start | bytes 393220
  1.4 1.4 %copy-start.2 = (bf16[256,256]{1,0:T(8,128)(2,1)S(1)}, bf16[256,256]{1,0:T(8,128)(2,1)}, u32[]{:S(2)}) copy-start(bf16[256,256]{1,0:T(8,128)(2,1)} %constant.13.clone.fwd_tail) | copy-start | bytes 393220
  1.5 1.4 %copy-start.3 = (f32[2,64,128]{2,1,0:T(8,128)S(1)}, f32[2,64,128]{2,1,0:T(8,128)}, u32[]{:S(2)}) copy-start(f32[2,64,128]{2,1,0:T(8,128)} %constant.17.clone.twist) | copy-start | bytes 196612
  1.5 1.3 %copy-start.4 = (bf16[128,128]{1,0:T(8,128)(2,1)S(1)}, bf16[128,128]{1,0:T(8,128)(2,1)}, u32[]{:S(2)}) copy-start(bf16[128,128]{1,0:T(8,128)(2,1)} %constant.12.clone.fwd_lead) | copy-start | bytes 98308
  1.5 1.3 %copy-start.5 = (bf16[18,128]{1,0:T(8,128)(2,1)S(1)}, bf16[18,128]{1,0:T(8,128)(2,1)}, u32[]{:S(2)}) copy-start(bf16[18,128]{1,0:T(8,128)(2,1)} %constant.15.clone.inv_lead) | copy-start | bytes 13828
  2.8 0.7 %copy-start.6 = (s32[128]{0:T(128)S(1)}, s32[128]{0:T(128)}, u32[]{:S(2)}) copy-start(s32[128]{0:T(128)} %param.13) | copy-start | bytes 1540
  2.8 0.7 %copy-start.7 = (s32[128]{0:T(128)S(1)}, s32[128]{0:T(128)}, u32[]{:S(2)}) copy-start(s32[128]{0:T(128)} %param.14) | copy-start | bytes 1540

commit v3 on v2

--- a/solution.py
+++ b/solution.py
@@ -64,6 +64,23 @@
     peers = [sibling, *[across(step) for step in range(1, chips)], *[{"az": along(step)} for step in range(1, az_count)]]
     for peer in peers:
         pl.semaphore_signal(barrier, inc=1, device_id=peer, device_id_type=MESH)
+
+    entries = taps.shape[1]
+    chooser = (lax.broadcasted_iota(jnp.int32, (entries, slab), 0) == index[...]).astype(jnp.bfloat16)
+    tap_rows = jnp.dot(taps[...].astype(jnp.bfloat16), chooser, preferred_element_type=jnp.float32)
+    tap_count = tap_rows.shape[0]
+    reach = slab + TAIL
+    offset = (
+        lax.broadcasted_iota(jnp.int32, (reach, slab), 0)
+        - lax.broadcasted_iota(jnp.int32, (reach, slab), 1)
+        - (HALO - tap_count // 2)
+        - shift[...]
+    )
+    band = jnp.zeros((reach, slab), jnp.float32)
+    for tap in range(tap_count):
+        band = jnp.where(offset == tap, tap_rows[tap : tap + 1, :], band)
+    band = band.astype(jnp.bfloat16)
+
     pl.semaphore_wait(barrier, len(peers))
 
     started = []
@@ -80,6 +97,27 @@
         send(sig.at[:, pl.ds(other * half + pos * part, part)], mate.at[pos], send_a.at[pos], recv_a.at[pos], sibling)
         for pos in range(chunks)
     ]
+    twist_real, twist_imag = twist[0], twist[1]
+
+    def forward(blocks):
+        step = jnp.dot(fwd_lead[...], jnp.concatenate(blocks, axis=1), preferred_element_type=jnp.float32)
+        turned = []
+        for pos in range(len(blocks)):
+            real = step[:lead, pos * TAIL : (pos + 1) * TAIL]
+            imag = step[lead:, pos * TAIL : (pos + 1) * TAIL]
+            turned.append(
+                jnp.concatenate(
+                    [real * twist_real - imag * twist_imag, real * twist_imag + imag * twist_real], axis=1
+                ).astype(jnp.bfloat16)
+            )
+        return jnp.dot(jnp.concatenate(turned, axis=0), fwd_tail[...], preferred_element_type=jnp.float32)
+
+    def stacked(block):
+        return [jnp.concatenate([block[0, pos], block[1, pos]], axis=0) for pos in range(block.shape[1])]
+
+    early = chunks // 2
+    spec[0, :early] = forward(stacked(sig[:, : early * part])).reshape(early, part * lead, 2 * TAIL)
+
     chosen_side, chosen_chip = lax.rem(source[0], 2), source[0] // 2
     second = []
     for pos in range(chunks):
@@ -95,43 +133,8 @@
             ]
         )
 
-    twist_real, twist_imag = twist[0], twist[1]
-
-    def forward(blocks):
-        step = jnp.dot(fwd_lead[...], jnp.concatenate(blocks, axis=1), preferred_element_type=jnp.float32)
-        turned = []
-        for pos in range(len(blocks)):
-            real = step[:lead, pos * TAIL : (pos + 1) * TAIL]
-            imag = step[lead:, pos * TAIL : (pos + 1) * TAIL]
-            turned.append(
-                jnp.concatenate(
-                    [real * twist_real - imag * twist_imag, real * twist_imag + imag * twist_real], axis=1
-                ).astype(jnp.bfloat16)
-            )
-        return jnp.dot(jnp.concatenate(turned, axis=0), fwd_tail[...], preferred_element_type=jnp.float32)
-
-    def stacked(block):
-        return [jnp.concatenate([block[0, pos], block[1, pos]], axis=0) for pos in range(block.shape[1])]
-
-    spec[...] = forward(stacked(sig[...])).reshape(spec.shape)
-
-    entries = taps.shape[0]
-    chooser = (lax.broadcasted_iota(jnp.int32, (entries, slab), 0) == index[...]).astype(jnp.bfloat16)
-    tap_rows = lax.dot_general(
-        taps[...].astype(jnp.bfloat16), chooser, (((0,), (0,)), ((), ())), preferred_element_type=jnp.float32
-    )
-    tap_count = tap_rows.shape[0]
-    reach = slab + TAIL
-    offset = (
-        lax.broadcasted_iota(jnp.int32, (reach, slab), 0)
-        - lax.broadcasted_iota(jnp.int32, (reach, slab), 1)
-        - (HALO - tap_count // 2)
-        - shift[...]
-    )
-    band = jnp.zeros((reach, slab), jnp.float32)
-    for tap in range(tap_count):
-        band = jnp.where(offset == tap, tap_rows[tap : tap + 1, :], band)
-    band = band.astype(jnp.bfloat16)
+    spec[0, early:] = forward(stacked(sig[:, early * part : half])).reshape(chunks - early, part * lead, 2 * TAIL)
+    spec[1] = forward(stacked(sig[:, half:])).reshape(chunks, part * lead, 2 * TAIL)
 
     def backward(which, pos):
         weight = filt[which, pos].astype(jnp.float32)
@@ -161,19 +164,9 @@
                 ]
 
     fourth = []
-    for pos in range(chunks):
-        for copy in second[pos]:
-            copy.wait_recv()
-        chosen = cand[0, pos]
-        for place in range(1, chips):
-            chosen = jnp.where(chosen_chip == place, cand[place, pos], chosen)
-        ref = forward(stacked(chosen))
-        real, imag = ref[:, :TAIL], ref[:, TAIL:]
-        inverse = lax.rsqrt(jnp.maximum(real * real + imag * imag, 1.0))
-        filt[side, pos] = jnp.concatenate([real * inverse, -imag * inverse], axis=1).astype(jnp.bfloat16)
-        third = send(filt.at[side, pos], filt.at[side, pos], send_c.at[pos], recv_c.at[pos], sibling)
-        backward(side, pos)
-        third.wait_recv()
+
+    def finish(pos):
+        third[pos].wait_recv()
         backward(other, pos)
         if pos % per_group == per_group - 1:
             group = pos // per_group
@@ -196,6 +189,23 @@
                 ]
             )
             framed[group, me_az] = comp[group, pl.ds(me_az, 2)]
+
+    third = []
+    for pos in range(chunks):
+        for copy in second[pos]:
+            copy.wait_recv()
+        chosen = cand[0, pos]
+        for place in range(1, chips):
+            chosen = jnp.where(chosen_chip == place, cand[place, pos], chosen)
+        ref = forward(stacked(chosen))
+        real, imag = ref[:, :TAIL], ref[:, TAIL:]
+        inverse = lax.rsqrt(jnp.maximum(real * real + imag * imag, 1.0))
+        filt[side, pos] = jnp.concatenate([real * inverse, -imag * inverse], axis=1).astype(jnp.bfloat16)
+        third.append(send(filt.at[side, pos], filt.at[side, pos], send_c.at[pos], recv_c.at[pos], sibling))
+        if pos:
+            finish(pos - 1)
+        backward(side, pos)
+    finish(chunks - 1)
 
     aligned = []
     for group in range(groups):
@@ -254,7 +264,7 @@
         compiler_params=pltpu.CompilerParams(collective_id=0, has_side_effects=True, vmem_limit_bytes=48 * 2**20),
     )(
         sig,
-        tap_table,
+        tap_table.T,
         range_shift.reshape(1, slab),
         tap_index.reshape(1, slab),
         ref_channel,

time: 25.3 us -> 23.5 us (0.929)
  Pallas kernels: 21 us -> 20 us
  local copies, waits for them, and re-layouts: 3.32 us -> 2.56 us
    pallas_call x1, Pallas kernels: 21 us -> 20 us  [shards(): pl.pallas_call(functools.partial(kernel, chan_count, az_count, chunks, gr...]
    unnamed x19 -> x20, local copies, waits for them, and re-layouts: 3.32 us -> 2.56 us
where the time goes in v3:
time: 23.5 us; the launch traced here: 23.3 us
  Pallas kernels  20 us (85%)
  local copies, waits for them, and re-layouts  2.56 us (11%)
  between operations  0.8 us (3%)
    pallas_call x1, Pallas kernels, shards(): pl.pallas_call(functools.partial(kernel, chan_count, az_count, chunks, gr...  20 us
    unnamed x20, local copies, waits for them, and re-layouts  2.56 us

profile of v3, /device:TPU:0, one launch (start us, length us, event | category | flops | bytes accessed | tf_op | source)
XLA Modules:
  0.0 23.3 jit_solution(9191553221856230163)
XLA Ops:
  0.7 0.0 copy-start
  0.7 0.0 copy-start.1
  0.7 0.0 copy-start.2
  0.7 0.0 copy-start.3
  0.7 0.0 copy-start.4
  0.7 0.0 copy-start.5
  0.7 0.0 copy-start.6
  0.7 1.3 %copy.12 = bf16[4,8,64,128]{3,2,1,0:T(8,128)(2,1)S(1)} copy(bf16[4,8,64,128]{3,1,2,0:T(8,128)(2,1)} %bitcast.14) | data formatting | bytes 1048576
  2.0 0.0 copy-start.7
  2.0 0.0 copy-start.8
  2.0 0.0 copy-done
  2.0 0.0 copy-done.1
  2.1 0.0 copy-done.2
  2.1 0.0 copy-done.3
  2.1 0.0 copy-done.4
  2.1 0.0 copy-done.5
  2.1 0.0 copy-done.6
  2.1 0.6 %copy-done.7 = s32[128]{0:T(128)S(1)} copy-done((s32[128]{0:T(128)S(1)}, s32[128]{0:T(128)}, u32[]{:S(2)}) %copy-start.7) | copy-done | bytes 536
  2.7 0.0 copy-done.8
  2.7 20.0 %shard_map.109 = f32[256,128]{1,0:T(8,128)S(1)} custom-call(bf16[2,16,64,128]{3,2,1,0:T(8,128)(2,1)S(1)} %bitcast.9, f32[16,64]{1,0:T(8,128)S(1)} %bitcast.11, s32[1,128]{1,0:T(1,128)S(1)} %bitcast.12, s32[1,128]{1,0:T(1,128)S(1)} %bitcast.13, s32[1]{0:T(128)S(6)} %copy.14.source, bf16[128,128]{1,0:T(8,128)(2,1)S(1)} %copy-done.4, ...), custom_call_target="tpu_custom_call" | custom-call | tf_op jit(solution)/shard_map/pallas_call | solution.py:242
  22.7 0.7 %copy.15 = f32[1,2,128,128]{3,2,1,0:T(8,128)} copy(f32[1,2,128,128]{3,2,1,0:T(8,128)S(1)} %bitcast.10) | data formatting | bytes 262144
Async XLA Ops:
  0.7 1.4 %copy-start = (bf16[256,256]{1,0:T(8,128)(2,1)S(1)}, bf16[256,256]{1,0:T(8,128)(2,1)}, u32[]{:S(2)}) copy-start(bf16[256,256]{1,0:T(8,128)(2,1)} %constant.16.clone.doppler) | copy-start | bytes 393220
  0.7 1.4 %copy-start.1 = (bf16[256,256]{1,0:T(8,128)(2,1)S(1)}, bf16[256,256]{1,0:T(8,128)(2,1)}, u32[]{:S(2)}) copy-start(bf16[256,256]{1,0:T(8,128)(2,1)} %constant.14.clone.inv_tail) | copy-start | bytes 393220
  0.7 1.4 %copy-start.2 = (bf16[256,256]{1,0:T(8,128)(2,1)S(1)}, bf16[256,256]{1,0:T(8,128)(2,1)}, u32[]{:S(2)}) copy-start(bf16[256,256]{1,0:T(8,128)(2,1)} %constant.13.clone.fwd_tail) | copy-start | bytes 393220
  0.7 1.4 %copy-start.3 = (f32[2,64,128]{2,1,0:T(8,128)S(1)}, f32[2,64,128]{2,1,0:T(8,128)}, u32[]{:S(2)}) copy-start(f32[2,64,128]{2,1,0:T(8,128)} %constant.17.clone.twist) | copy-start | bytes 196612
  0.7 1.4 %copy-start.4 = (bf16[128,128]{1,0:T(8,128)(2,1)S(1)}, bf16[128,128]{1,0:T(8,128)(2,1)}, u32[]{:S(2)}) copy-start(bf16[128,128]{1,0:T(8,128)(2,1)} %constant.12.clone.fwd_lead) | copy-start | bytes 98308
  0.7 1.4 %copy-start.5 = (f32[64,16]{0,1:T(8,128)S(1)}, f32[64,16]{0,1:T(8,128)}, u32[]{:S(2)}) copy-start(f32[64,16]{0,1:T(8,128)} %param.12) | copy-start | bytes 12292
  0.7 1.4 %copy-start.6 = (bf16[18,128]{1,0:T(8,128)(2,1)S(1)}, bf16[18,128]{1,0:T(8,128)(2,1)}, u32[]{:S(2)}) copy-start(bf16[18,128]{1,0:T(8,128)(2,1)} %constant.15.clone.inv_lead) | copy-start | bytes 13828
  2.0 0.7 %copy-start.7 = (s32[128]{0:T(128)S(1)}, s32[128]{0:T(128)}, u32[]{:S(2)}) copy-start(s32[128]{0:T(128)} %param.13) | copy-start | bytes 1540
  2.0 0.7 %copy-start.8 = (s32[128]{0:T(128)S(1)}, s32[128]{0:T(128)}, u32[]{:S(2)}) copy-start(s32[128]{0:T(128)} %param.14) | copy-start | bytes 1540
